TPU v7x, 32 devices: a whole 2x2x4 slice. The times are simulated.
32 devices in a mesh: groups: 2 (over y), ep: 4 (over x, core), tp: 4 (over z).
Axes of the slice: x: 2, y: 2, z: 4, core: 2. Of those that a mesh axis runs over, the one named last changes fastest.
Arguments:
- hidden_states: bfloat16 [256, 7168], P(('groups', 'ep', 'tp')), parts along dimension 0, may hold values from -6 to 6
- norm_gain: float32 [7168], replicated, may hold values from 0.1 to 1.9
- expert_ids: int32 [256, 8], P(('groups', 'ep', 'tp')), parts along dimension 0, may hold values from 0 to 15, all different within a row; in each aligned block of 8 rows (0 to 7, 8 to 15, ...) at most 5 rows name the same one
- gate_weights: float32 [256, 8], P(('groups', 'ep', 'tp')), parts along dimension 0, may hold values from 0.1 to 1
- capacity: int32 [16], replicated, may hold values from 3 to 5
- expert_in: bfloat16 [16, 2048, 2, 7168], P('ep', 'tp'), may hold values from -0.0625 to 0.0625
- expert_out: bfloat16 [16, 2048, 7168], P('ep', 'tp'), may hold values from -0.125 to 0.125
Outputs:
- mixed_out: bfloat16 [256, 7168], P(('groups', 'ep', 'tp')), parts along dimension 0
There are 2 independent parts, one for each index of `groups`. A program takes and returns all parts, laid end to end along the dimension named above; an argument that names none is the same for every part. Nothing has to cross between parts.
Inputs may be any that keep to these rules, and one draw needn't show every extreme that they name: `expert_ids`: each row names 8 different experts; within the rows of one device no expert is named more than 5 times.
All inputs are finite; a program needn't handle non-finite values.
Results may differ from a plain program's by a relative error of at most 0.006.
Values may be sent and summed in bfloat16 or wider, within the bound.
A program may use at most 320 MiB of HBM per device.

v0:
```python
import jax
import jax.numpy as jnp
from jax import lax
from jax.sharding import PartitionSpec as P

CAP = 5


EPSILON = 1e-06


def expert_terms(received, weight_in, weight_out):
    group_part, slot_part, local_count, model_width = received.shape
    row_block = received.reshape(group_part * slot_part, local_count, model_width)
    gate_part = jnp.einsum(
        "rld,lfd->rlf", row_block, weight_in[:, :, 0], preferred_element_type=jnp.float32
    )
    up_part = jnp.einsum(
        "rld,lfd->rlf", row_block, weight_in[:, :, 1], preferred_element_type=jnp.float32
    )
    hidden = (jax.nn.silu(gate_part) * up_part).astype(jnp.bfloat16)
    product = jnp.einsum("rlf,lfd->rld", hidden, weight_out, preferred_element_type=jnp.float32)
    return product.reshape(group_part, slot_part, local_count, model_width)


def shards(hidden_states, norm_gain, expert_ids, gate_weights, capacity, expert_in, expert_out):
    group_size = lax.axis_size("ep")
    split_size = lax.axis_size("tp")
    token_count, model_width = hidden_states.shape
    top_count = expert_ids.shape[1]
    expert_count = capacity.shape[0]
    local_count = expert_in.shape[0]
    slot_count = CAP
    values = hidden_states.astype(jnp.float32)
    inverse = lax.rsqrt(jnp.mean(values * values, axis=1, keepdims=True) + EPSILON)
    normed = (values * inverse * norm_gain).astype(jnp.bfloat16)
    route_ids = expert_ids.reshape(-1)
    onehot = (route_ids[:, None] == jnp.arange(expert_count, dtype=jnp.int32)[None, :]).astype(
        jnp.int32
    )
    before = jnp.sum((jnp.cumsum(onehot, axis=0) - onehot) * onehot, axis=1)
    allowed = jnp.sum(onehot * capacity[None, :], axis=1)
    keeping = before < allowed
    position = (
        route_ids // local_count * slot_count + before
    ) * local_count + route_ids % local_count
    buffer_size = expert_count * slot_count
    placing = (
        (position[:, None] == jnp.arange(buffer_size, dtype=jnp.int32)[None, :]) & keeping[:, None]
    ).astype(jnp.float32)
    route_token = jnp.arange(route_ids.shape[0], dtype=jnp.int32)[:, None] // top_count
    owning = (route_token == jnp.arange(token_count, dtype=jnp.int32)[None, :]).astype(jnp.float32)
    spreading = jnp.dot(placing.T, owning, precision=lax.Precision.HIGHEST).astype(jnp.bfloat16)
    outgoing = jnp.dot(spreading, normed, preferred_element_type=jnp.float32).astype(jnp.bfloat16)
    outgoing = outgoing.reshape(group_size, slot_count, local_count, model_width)
    weighting = placing * gate_weights.reshape(-1)[:, None]
    combining = jnp.dot(owning.T, weighting, precision=lax.Precision.HIGHEST)
    copies = jnp.broadcast_to(
        outgoing[:, None], (group_size, split_size, slot_count, local_count, model_width)
    )
    copies = copies.reshape(group_size * split_size, slot_count, local_count, model_width)
    partial_value = expert_terms(
        lax.all_to_all(copies, ("ep", "tp"), split_axis=0, concat_axis=0, tiled=True),
        expert_in,
        expert_out,
    )
    partial_value = partial_value.reshape(
        group_size, split_size, slot_count, local_count, model_width
    )
    flat_partial = partial_value.reshape(
        group_size * split_size, slot_count, local_count, model_width
    )
    pieces_back = lax.all_to_all(
        flat_partial, ("ep", "tp"), split_axis=0, concat_axis=0, tiled=True
    )
    summed = jnp.sum(
        pieces_back.reshape(group_size, split_size, slot_count, local_count, model_width), axis=1
    )
    returned = summed.astype(jnp.bfloat16)
    flat_back = returned.reshape(buffer_size, model_width).astype(jnp.float32)
    mixed_out = values + jnp.dot(combining, flat_back, precision=lax.Precision.HIGHEST)
    return mixed_out.astype(jnp.bfloat16)


def solution(mesh):
    in_specs = (
        P(("groups", "ep", "tp"), None),
        P(),
        P(("groups", "ep", "tp"), None),
        P(("groups", "ep", "tp"), None),
        P(),
        P("ep", "tp", None, None),
        P("ep", "tp", None),
    )
    out_specs = P(("groups", "ep", "tp"), None)
    return jax.shard_map(shards, mesh=mesh, in_specs=in_specs, out_specs=out_specs, check_vma=False)
```

profile of v0, /device:TPU:0, one launch (start us, length us, event | category | flops | bytes accessed | tf_op | source)
XLA Modules:
  0.0 436.7 jit_solution(10164100546282936844)
XLA Ops:
  0.0 0.8 reshape.124
  0.8 0.1 fusion.27
  0.8 0.1 reduce_window_sum.11
  0.9 0.8 select_reduce_fusion
  1.8 0.0 copy-start.2
  1.8 0.0 copy-start.4
  1.8 0.0 copy-start.6
  1.9 1.1 fusion.19
  2.9 0.0 copy-done.2
  2.9 0.0 copy-done.4
  2.9 0.0 copy-done.6
  3.0 0.3 convolution_convert_fusion.1
  3.2 1.4 convolution_convert_fusion
  4.6 0.5 broadcast_in_dim.4
  5.1 3.6 broadcast_in_dim.5
  8.7 7.4 %all-to-all-start = ((bf16[16,5,4,7168]{3,2,1,0:T(4,128)(2,1)}), bf16[16,5,4,7168]{3,2,1,0:T(4,128)(2,1)}, u32[]{:S(2)}, u32[]{:S(2)}) async-start(bf16[16,5,4,7168]{3,2,1,0:T(4,128)(2,1)} %bitcast.47), calls=%async_computation | async-start | bytes 9175040 | tf_op jit(solution)/shard_map/all_to_all | solution.py:63
  16.2 109.8 %fusion.42 = (bf16[4,512,1,7168]{3,2,1,0:T(2,128)(2,1)}, bf16[4,512,1,7168]{3,2,1,0:T(2,128)(2,1)}) fusion(bf16[4,512,2,7168]{3,2,1,0:T(2,128)(2,1)} %param.12), kind=kLoop, calls=%fused_computation.53 | loop fusion | bytes 117440512 | tf_op jit(solution)/shard_map/slice | solution.py:16
  126.0 0.0 all-to-all-done
  126.0 39.2 %fusion.5 = f32[80,4,512]{2,0,1:T(8,128)S(1)} fusion(bf16[4,512,1,7168]{3,2,1,0:T(2,128)(2,1)} %get-tuple-element.7, bf16[80,4,7168]{2,1,0:T(4,128)(2,1)} %bitcast.1), kind=kOutput, calls=%fused_computation.11 | convolution fusion | flops 2348810240 | bytes 34603008 | tf_op jit(solution)/shard_map/rld,lfd->rlf/dot_general | solution.py:15
  165.2 25.6 %fusion.14.clone.4 = bf16[80,4,512]{2,0,1:T(8,128)(2,1)S(1)} fusion(bf16[4,512,1,7168]{3,2,1,0:T(2,128)(2,1)} %get-tuple-element.8, bf16[80,4,7168]{2,1,0:T(4,128)(2,1)} %bitcast.1, f32[80,4,512]{2,0,1:T(8,128)S(1)} %fusion.5), kind=kOutput, calls=%fused_computation.14.clone.clone.clone.1 | convolution fusion | flops 2349793280 | bytes 34930688 | tf_op jit(solution)/shard_map/rld,lfd->rlf/dot_general | solution.py:18
  190.8 18.1 %convolution_bitcast_fusion = f32[80,4,7168]{2,0,1:T(8,128)} fusion(bf16[4,512,7168]{2,1,0:T(8,128)(2,1)} %param.13, bf16[80,4,512]{2,0,1:T(8,128)(2,1)S(1)} %fusion.14.clone.4), kind=kOutput, calls=%fused_computation.4 | convolution fusion | flops 2348810240 | bytes 38862848 | tf_op jit(solution)/shard_map/rlf,lfd->rld/dot_general | solution.py:22
  208.8 13.0 %copy.13 = f32[80,4,7168]{2,1,0:T(4,128)} copy(f32[80,4,7168]{2,0,1:T(8,128)} %convolution_bitcast_fusion) | data formatting | bytes 18350080 | tf_op jit(solution)/shard_map/rlf,lfd->rld/transpose | solution.py:22
  221.9 0.0 copy-start.1
  221.9 0.0 copy-start.3
  221.9 0.0 copy-start.5
  221.9 0.0 copy-start.7
  221.9 6.1 %all-to-all-start.1 = ((f32[16,5,4,7168]{3,2,1,0:T(4,128)}), f32[16,5,4,7168]{3,2,1,0:T(4,128)}, u32[]{:S(2)}, u32[]{:S(2)}) async-start(f32[16,5,4,7168]{3,2,1,0:T(4,128)} %bitcast.46), calls=%async_computation.1 | async-start | bytes 18350080 | tf_op jit(solution)/shard_map/all_to_all | solution.py:73
  228.0 0.0 copy-done.1
  228.1 0.0 copy-start
  228.1 0.1 mul.71
  228.1 0.0 copy-done.3
  228.1 0.0 copy-done.5
  228.2 0.0 copy-done.7
  228.2 0.3 fusion.25
  228.4 200.7 %all-to-all-done.1 = f32[16,5,4,7168]{3,2,1,0:T(4,128)} async-done(((f32[16,5,4,7168]{3,2,1,0:T(4,128)}), f32[16,5,4,7168]{3,2,1,0:T(4,128)}, u32[]{:S(2)}, u32[]{:S(2)}) %all-to-all-start.1) | async-done | bytes 9175072 | tf_op jit(solution)/shard_map/all_to_all | solution.py:73
  429.1 6.1 %bitcast_reduce_fusion = bf16[4,5,4,7168]{3,2,1,0:T(4,128)(2,1)S(1)} fusion(f32[16,5,4,7168]{3,2,1,0:T(4,128)} %all-to-all-done.1), kind=kLoop, calls=%fused_computation.5 | loop fusion | flops 1720320 | bytes 10321920 | tf_op jit(solution)/shard_map/reduce_sum | solution.py:76
  435.2 0.3 convert_element_type.38
  435.5 0.0 copy-done
  435.5 1.2 fusion.2
  (3 shorter events, 0.0 us)
Async XLA Ops:
  1.8 1.1 copy-start.2
  1.8 1.1 copy-start.4
  1.8 1.1 copy-start.6
  8.7 117.2 %all-to-all-start = ((bf16[16,5,4,7168]{3,2,1,0:T(4,128)(2,1)}), bf16[16,5,4,7168]{3,2,1,0:T(4,128)(2,1)}, u32[]{:S(2)}, u32[]{:S(2)}) async-start(bf16[16,5,4,7168]{3,2,1,0:T(4,128)(2,1)} %bitcast.47), calls=%async_computation | async-start | bytes 9175040 | tf_op jit(solution)/shard_map/all_to_all | solution.py:63
  221.9 6.2 %copy-start.1 = (f32[8,8]{1,0:T(8,128)S(1)}, f32[8,8]{1,0:T(8,128)}, u32[]{:S(2)}) copy-start(f32[8,8]{1,0:T(8,128)} %param.10) | copy-start | bytes 772
  221.9 6.3 %copy-start.3 = (s32[64]{0:T(128)S(1)}, s32[64]{0:T(128)}, u32[]{:S(2)}) copy-start(s32[64]{0:T(128)} %copy-done.2) | copy-start | bytes 772
  221.9 6.3 %copy-start.5 = (s32[64]{0:T(128)S(1)}, s32[64]{0:T(128)}, u32[]{:S(2)}) copy-start(s32[64]{0:T(128)} %copy-done.4) | copy-start | bytes 772
  221.9 6.3 %copy-start.7 = (pred[64]{0:T(512)(128)(4,1)S(1)}, pred[64]{0:T(512)(128)(4,1)}, u32[]{:S(2)}) copy-start(pred[64]{0:T(512)(128)(4,1)} %copy-done.6) | copy-start | bytes 196
  221.9 207.2 %all-to-all-start.1 = ((f32[16,5,4,7168]{3,2,1,0:T(4,128)}), f32[16,5,4,7168]{3,2,1,0:T(4,128)}, u32[]{:S(2)}, u32[]{:S(2)}) async-start(f32[16,5,4,7168]{3,2,1,0:T(4,128)} %bitcast.46), calls=%async_computation.1 | async-start | bytes 18350080 | tf_op jit(solution)/shard_map/all_to_all | solution.py:73
  228.1 207.4 %copy-start = (bf16[8,7168]{1,0:T(8,128)(2,1)S(1)}, bf16[8,7168]{1,0:T(8,128)(2,1)}, u32[]{:S(2)}) copy-start(bf16[8,7168]{1,0:T(8,128)(2,1)} %param.7) | copy-start | bytes 344068
where the time goes:
time: 437 us
  waiting for transfers between devices  201 us (46%)
  local copies, waits for them, and re-layouts  128 us (29%)
  matrix products  86 us (20%)
  starting transfers between devices  13.6 us (3%)
  other arithmetic  8.18 us (2%)
    all_to_all x1, waiting for transfers between devices, shards(): lax.all_to_all(flat_partial, ('ep', 'tp'), split_axis=0, concat_axis=0, t...  201 us
    slice x1, local copies, waits for them, and re-layouts, expert_terms(): weight_in[:, :, 0]  110 us
    dot_general x1, matrix products, expert_terms(): jnp.einsum('rld,lfd->rlf', row_block, weight_in[:, :, 0], preferred_eleme...  39.2 us
    dot_general x1, matrix products, expert_terms(): jnp.einsum('rld,lfd->rlf', row_block, weight_in[:, :, 1], preferred_eleme...  25.6 us
    dot_general x1, matrix products, expert_terms(): jnp.einsum('rlf,lfd->rld', hidden, weight_out, preferred_element_type=jnp...  18.1 us
    transpose x1, local copies, waits for them, and re-layouts, expert_terms(): jnp.einsum('rlf,lfd->rld', hidden, weight_out, preferred_element_type=jnp...  13 us
  transfers between devices with their start and end apart: 2, of which 1 were waited for; matrix products, arithmetic and copies ran while one was open for 25% of the time, Pallas kernels for 0%

commit v1 on v0

v1 whole, which is shorter than its diff:
```python
import functools
import jax
import jax.numpy as jnp
from jax import lax
from jax.experimental import pallas as pl
from jax.experimental.pallas import tpu as pltpu
from jax.sharding import PartitionSpec as P

EPSILON = 1e-06
ROWS = 128


def experts_kernel(x_ref, w_ref, in_hbm, out_w_ref, o_ref, stage, pair, total, sems):
    e, f = pl.program_id(1), pl.program_id(2)
    n_e, n_f = pl.num_programs(1), pl.num_programs(2)
    step = e * n_f + f
    last = n_e * n_f
    block = stage.shape[1]
    flat = in_hbm.reshape(in_hbm.shape[0] * in_hbm.shape[1] * 2, in_hbm.shape[3])

    def fetch(at):
        return pltpu.make_async_copy(
            flat.at[pl.ds(pl.multiple_of(at * block, block), block)], stage.at[at % 2], sems.at[at % 2]
        )

    @pl.when(step == 0)
    def _():
        fetch(step).start()

    @pl.when(step + 1 < last)
    def _():
        fetch(step + 1).start()

    fetch(step).wait()
    pair[...] = lax.dot_general(
        stage[step % 2], x_ref[...], (((1,), (1,)), ((), ())), preferred_element_type=jnp.float32
    )
    half = block // 2
    gate = pair[pl.ds(0, half, stride=2), :]
    up = pair[pl.ds(1, half, stride=2), :]
    scale = w_ref[pl.ds(e, 1), :]
    hidden = gate / (1.0 + jnp.exp(-gate)) * up * scale
    hidden = hidden.T.astype(jnp.bfloat16)
    part = jnp.dot(hidden, out_w_ref[0], preferred_element_type=jnp.float32)

    @pl.when(step == 0)
    def _():
        total[...] = part

    @pl.when(step > 0)
    def _():
        total[...] += part

    @pl.when(step == last - 1)
    def _():
        o_ref[...] = total[...].astype(o_ref.dtype)


def experts(x, weights, expert_in, expert_out):
    count, width = x.shape
    n_e, n_f = expert_in.shape[:2]
    block = min(256, n_f)
    return pl.pallas_call(
        experts_kernel,
        grid=(count // ROWS, n_e, n_f // block),
        out_shape=jax.ShapeDtypeStruct((count, width), jnp.bfloat16),
        in_specs=[
            pl.BlockSpec((ROWS, width), lambda t, e, f: (t, 0)),
            pl.BlockSpec((weights.shape[0], ROWS), lambda t, e, f: (0, t)),
            pl.BlockSpec(memory_space=pl.ANY),
            pl.BlockSpec((1, block, width), lambda t, e, f: (e, f, 0)),
        ],
        out_specs=pl.BlockSpec((ROWS, width), lambda t, e, f: (t, 0)),
        scratch_shapes=[
            pltpu.VMEM((2, 2 * block, width), jnp.bfloat16),
            pltpu.VMEM((2 * block, ROWS), jnp.float32),
            pltpu.VMEM((ROWS, width), jnp.float32),
            pltpu.SemaphoreType.DMA((2,)),
        ],
        compiler_params=pltpu.CompilerParams(vmem_limit_bytes=60 * 2**20),
    )(x, weights, expert_in, expert_out)


def shards(hidden_states, norm_gain, expert_ids, gate_weights, capacity, expert_in, expert_out):
    token_count, width = hidden_states.shape
    expert_count = capacity.shape[0]
    local_count = expert_in.shape[0]
    values = hidden_states.astype(jnp.float32)
    inverse = lax.rsqrt(jnp.mean(values * values, axis=1, keepdims=True) + EPSILON)
    normed = (values * inverse * norm_gain).astype(jnp.bfloat16)
    lanes = jnp.arange(expert_count, dtype=jnp.int32)
    chosen = (expert_ids[:, :, None] == lanes).astype(jnp.float32)
    named = jnp.sum(chosen, axis=1)
    lower = jnp.tril(jnp.ones((token_count, token_count), jnp.float32), -1)
    before = jnp.dot(lower, named, precision=lax.Precision.HIGHEST)
    kept = before < capacity[None, :].astype(jnp.float32)
    gates = jnp.where(kept, jnp.sum(chosen * gate_weights[:, :, None], axis=1), 0.0)
    high = gates.astype(jnp.bfloat16)
    low = (gates - high.astype(jnp.float32)).astype(jnp.bfloat16)
    pad = jnp.zeros((token_count, 128 - 2 * expert_count), jnp.bfloat16)
    sent = jnp.concatenate([normed, high, low, pad], axis=1)
    gathered = lax.all_gather(sent, ("ep", "tp"), axis=0, tiled=True)
    x = gathered[:, :width]
    high = gathered[:, width : width + expert_count].astype(jnp.float32)
    low = gathered[:, width + expert_count : width + 2 * expert_count].astype(jnp.float32)
    mine = lax.dynamic_slice_in_dim(high + low, lax.axis_index("ep") * local_count, local_count, 1)
    part = experts(x, mine.T, expert_in, expert_out)
    summed = lax.psum_scatter(part, ("ep", "tp"), scatter_dimension=0, tiled=True)
    return (values + summed.astype(jnp.float32)).astype(jnp.bfloat16)


def solution(mesh):
    in_specs = (
        P(("groups", "ep", "tp"), None),
        P(),
        P(("groups", "ep", "tp"), None),
        P(("groups", "ep", "tp"), None),
        P(),
        P("ep", "tp", None, None),
        P("ep", "tp", None),
    )
    out_specs = P(("groups", "ep", "tp"), None)
    return jax.shard_map(shards, mesh=mesh, in_specs=in_specs, out_specs=out_specs, check_vma=False)
```

time: 437 us -> 168 us (0.38)
  local copies, waits for them, and re-layouts: 128 us -> 4.74 us
  waiting for transfers between devices: 201 us -> 103 us
  matrix products: 86 us -> 0.2 us
  Pallas kernels: 0 us -> 40.1 us
  starting transfers between devices: 13.6 us -> 0.04 us
  between operations: 0.18 us -> 13.5 us
    all_to_all x2 -> x0, waiting for transfers between devices: 201 us -> none  [the longest x1 201 us: shards(): lax.all_to_all(flat_partial, ('ep', 'tp'), split_axis=0, concat_axis=0, t...]
    slice x1 -> x2, local copies, waits for them, and re-layouts: 110 us -> 3.74 us  [the longest x1 2.83 us: shards(): x = gathered[:, :width]]
    dot_general x7 -> x1, matrix products: 86 us -> 0.2 us  [shards(): before = jnp.dot(lower, named, precision=lax.Precision.HIGHEST)]
    reduce_scatter x0 -> x1, waiting for transfers between devices: none -> 59.8 us  [shards(): lax.psum_scatter(part, ('ep', 'tp'), scatter_dimension=0, tiled=True)]
    all_gather x0 -> x1, waiting for transfers between devices: none -> 43.5 us  [shards(): gathered = lax.all_gather(sent, ('ep', 'tp'), axis=0, tiled=True)]
    pallas_call x0 -> x1, Pallas kernels: none -> 40.1 us  [experts(): pl.pallas_call(experts_kernel, grid=(count // ROWS, n_e, n_f // block), o...]
    all_to_all x2 -> x0, starting transfers between devices: 13.6 us -> none  [the longest x1 7.44 us: shards(): lax.all_to_all(copies, ('ep', 'tp'), split_axis=0, concat_axis=0, tiled=T...]
    transpose x1 -> x0, local copies, waits for them, and re-layouts: 13 us -> none  [expert_terms(): jnp.einsum('rlf,lfd->rld', hidden, weight_out, preferred_element_type=jnp...]
  transfers between devices with their start and end apart: 2 -> 2, of which waited for: 1 -> 2; matrix products, arithmetic and copies ran while one was open for 25% -> 0% of each run, Pallas kernels for 0% -> 0%
where the time goes in v1:
time: 168 us
  waiting for transfers between devices  103 us (61%)
  Pallas kernels  40.1 us (24%)
  between operations  13.5 us (8%)
  other arithmetic  5.72 us (3%)
  local copies, waits for them, and re-layouts  4.74 us (3%)
    reduce_scatter x1, waiting for transfers between devices, shards(): lax.psum_scatter(part, ('ep', 'tp'), scatter_dimension=0, tiled=True)  59.8 us
    all_gather x1, waiting for transfers between devices, shards(): gathered = lax.all_gather(sent, ('ep', 'tp'), axis=0, tiled=True)  43.5 us
    pallas_call x1, Pallas kernels, experts(): pl.pallas_call(experts_kernel, grid=(count // ROWS, n_e, n_f // block), o...  40.1 us
  transfers between devices with their start and end apart: 2, of which 2 were waited for; matrix products, arithmetic and copies ran while one was open for 0% of the time, Pallas kernels for 0%

profile of v1, /device:TPU:0, one launch (start us, length us, event | category | flops | bytes accessed | tf_op | source)
XLA Modules:
  0.0 167.5 jit_solution(12607050097396892383)
XLA Ops:
  6.5 0.0 all-gather.2.cloned.1.call-start
  6.5 0.7 convert_element_type.37
  7.2 1.1 fusion.1
  8.3 0.8 convert_reduce_fusion
  9.1 1.0 fusion.3
  10.1 0.2 subtract_convert_fusion
  10.3 0.7 concatenate.3
  11.0 0.0 all-gather.2.cloned.1.call-update
  11.1 0.0 reduce-scatter.4.cloned.1.call-start
  11.1 43.5 %all-gather.2.cloned.1.call-done = bf16[128,7296]{1,0:T(8,128)(2,1)} async-done(((bf16[8,7296]{1,0:T(8,128)(2,1)}), bf16[128,7296]{1,0:T(8,128)(2,1)}) %all-gather.2.cloned.1.call-update) | async-done | bytes 1867792 | tf_op jit(solution)/shard_map/all_gather | solution.py:102
  54.6 0.9 fusion.11
  55.5 0.1 constant_dynamic-slice_fusion
  55.6 0.1 copy.35
  55.7 0.1 copy.36
  55.8 0.6 add_bitcast_fusion.w_ref
  56.4 2.8 %slice.12.x_ref = bf16[128,7168]{1,0:T(8,128)(2,1)} slice(bf16[128,7296]{1,0:T(8,128)(2,1)} %all-gather.2.cloned.1.call-done), slice={[0:128], [0:7168]} | slice | bytes 3670016 | tf_op jit(solution)/shard_map/slice | solution.py:103
  59.2 40.1 %shard_map.73 = bf16[128,7168]{1,0:T(8,128)(2,1)} custom-call(bf16[128,7168]{1,0:T(8,128)(2,1)} %slice.12.x_ref, f32[4,128]{1,0:T(4,128)} %add_bitcast_fusion.w_ref, bf16[4,512,2,7168]{3,2,1,0:T(2,128)(2,1)} %in_hbm.1, bf16[4,512,7168]{2,1,0:T(8,128)(2,1)} %out_w_ref.1), custom_call_target="tpu_custom_call" | custom-call | tf_op jit(solution)/shard_map/pallas_call | solution.py:63
  99.3 0.0 copy-start
  99.3 0.0 reduce-scatter.4.cloned.1.call-update
  99.4 59.8 %reduce-scatter.4.cloned.1.call-done = bf16[8,7168]{1,0:T(8,128)(2,1)} async-done(((bf16[128,7168]{1,0:T(8,128)(2,1)}), bf16[8,7168]{1,0:T(8,128)(2,1)}) %reduce-scatter.4.cloned.1.call-update) | async-done | bytes 114704 | tf_op jit(solution)/shard_map/reduce_scatter | solution.py:108
  159.1 0.0 copy-done
  159.1 1.6 fusion.4
  (3 shorter events, 0.0 us)
Async XLA Ops:
  6.5 48.1 %all-gather.2.cloned.1.call-start = ((), (), s32[]{:S(2)}) async-start(), calls=%async_computation.1 | async-start | bytes 1984512 | tf_op jit(solution)/shard_map/all_gather | solution.py:102
  11.1 148.1 %reduce-scatter.4.cloned.1.call-start = ((), (), s32[]{:S(2)}) async-start(), calls=%async_computation.2 | async-start | bytes 1949696 | tf_op jit(solution)/shard_map/reduce_scatter | solution.py:108
  99.3 59.8 %copy-start = (bf16[8,7168]{1,0:T(8,128)(2,1)S(1)}, bf16[8,7168]{1,0:T(8,128)(2,1)}, u32[]{:S(2)}) copy-start(bf16[8,7168]{1,0:T(8,128)(2,1)} %param.7) | copy-start | bytes 344068
Sparse Core Ops, SparseCore 0:
  11.2 43.4 all-gather.1
  99.5 59.5 reduce-scatter.3

commit v2 on v1

--- a/solution.py
+++ b/solution.py
@@ -1,4 +1,3 @@
-import functools
 import jax
 import jax.numpy as jnp
 from jax import lax
@@ -56,8 +55,8 @@
         o_ref[...] = total[...].astype(o_ref.dtype)
 
 
-def experts(x, weights, expert_in, expert_out):
-    count, width = x.shape
+def experts(x, width, weights, expert_in, expert_out):
+    count = x.shape[0]
     n_e, n_f = expert_in.shape[:2]
     block = min(256, n_f)
     return pl.pallas_call(
@@ -81,6 +80,162 @@
     )(x, weights, expert_in, expert_out)
 
 
+MESH = pl.DeviceIdType.MESH
+
+
+def places():
+    n_x, n_z = lax.axis_size("ep") // 2, lax.axis_size("tp")
+    ep, z = lax.axis_index("ep"), lax.axis_index("tp")
+    return n_x, n_z, ep // 2, ep % 2, z
+
+
+def greet(n_x, n_z, x, c, z):
+    barrier = pltpu.get_barrier_semaphore()
+    peers = [(x, 1 - c, z)]
+    peers += [((x + d) % n_x, c, z) for d in range(1, n_x)]
+    peers += [(x, c, (z + k) % n_z) for k in range(1, n_z)]
+    for px, pc, pz in peers:
+        pl.semaphore_signal(barrier, inc=1, device_id={"ep": px * 2 + pc, "tp": pz}, device_id_type=MESH)
+    pl.semaphore_wait(barrier, len(peers))
+
+
+def push(src, dst, sems, at, px, pc, pz):
+    return pltpu.make_async_remote_copy(
+        src_ref=src,
+        dst_ref=dst,
+        send_sem=sems[0].at[at],
+        recv_sem=sems[1].at[at],
+        device_id={"ep": px * 2 + pc, "tp": pz},
+        device_id_type=MESH,
+    )
+
+
+def gather_kernel(own_ref, out_ref, zs, zr, xs, xr, cs, cr):
+    n_x, n_z, x, c, z = places()
+    greet(n_x, n_z, x, c, z)
+    z_sems, x_sems, c_sems = (zs, zr), (xs, xr), (cs, cr)
+    sends = []
+
+    def send(*what):
+        copy = push(*what)
+        copy.start()
+        sends.append(copy)
+
+    def place(d, k):
+        return out_ref.at[(x - d + n_x) % n_x, c, (z - k + n_z) % n_z]
+
+    def other(d, k):
+        return out_ref.at[(x - d + n_x) % n_x, 1 - c, (z - k + n_z) % n_z]
+
+    mine = out_ref.at[x, c, z]
+    for k in range(1, n_z):
+        send(own_ref, mine, z_sems, k - 1, x, c, (z + k) % n_z)
+    for d in range(1, n_x):
+        send(own_ref, mine, x_sems, (d - 1) * n_z, (x + d) % n_x, c, z)
+    send(own_ref, mine, c_sems, 0, x, 1 - c, z)
+    out_ref[x, c, z] = own_ref[...]
+    for k in range(1, n_z):
+        here = place(0, k)
+        push(here, here, z_sems, k - 1, x, c, (z + k) % n_z).wait_recv()
+        for d in range(1, n_x):
+            send(here, here, x_sems, (d - 1) * n_z + k, (x + d) % n_x, c, z)
+        send(here, here, c_sems, k, x, 1 - c, z)
+    for k in range(n_z):
+        for d in range(1, n_x):
+            here = place(d, k)
+            push(here, here, x_sems, (d - 1) * n_z + k, (x + d) % n_x, c, z).wait_recv()
+            send(here, here, c_sems, d * n_z + k, x, 1 - c, z)
+    for d in range(n_x):
+        for k in range(n_z):
+            there = other(d, k)
+            push(there, there, c_sems, d * n_z + k, x, 1 - c, z).wait_recv()
+    for copy in sends:
+        copy.wait_send()
+
+
+def gather(own):
+    n_x, n_z = lax.axis_size("ep") // 2, lax.axis_size("tp")
+    rows, width = own.shape
+    sems = pltpu.SemaphoreType.DMA
+    out = pl.pallas_call(
+        gather_kernel,
+        out_shape=jax.ShapeDtypeStruct((n_x, 2, n_z, rows, width), own.dtype),
+        in_specs=[pl.BlockSpec(memory_space=pltpu.VMEM)],
+        out_specs=pl.BlockSpec(memory_space=pltpu.VMEM),
+        scratch_shapes=[sems((n_z,))] * 2 + [sems((n_x * n_z,))] * 4,
+        compiler_params=pltpu.CompilerParams(
+            collective_id=0, has_side_effects=True, vmem_limit_bytes=60 * 2**20
+        ),
+    )(own)
+    return out.reshape(n_x * 2 * n_z * rows, width)
+
+
+def scatter_kernel(part_ref, own_ref, out_ref, from_c, to_x, from_x, to_z, from_z, cs, cr, xs, xr, zs, zr):
+    n_x, n_z, x, c, z = places()
+    greet(n_x, n_z, x, c, z)
+    c_sems, x_sems, z_sems = (cs, cr), (xs, xr), (zs, zr)
+    sends = []
+
+    def send(*what):
+        copy = push(*what)
+        copy.start()
+        sends.append(copy)
+
+    turns = list(range(1, n_z)) + [0]
+    blocks = [(d, k) for d in list(range(1, n_x)) + [0] for k in turns]
+
+    def pair_copy(d, k, side):
+        src = part_ref.at[(x + d) % n_x, side, (z + k) % n_z]
+        return src, from_c.at[d * n_z + k], c_sems, d * n_z + k, x, 1 - c, z
+
+    for d, k in blocks:
+        send(*pair_copy(d, k, 1 - c))
+
+    def paired(d, k):
+        push(*pair_copy(d, k, 1 - c)).wait_recv()
+        near = part_ref[(x + d) % n_x, c, (z + k) % n_z].astype(jnp.float32)
+        return near + from_c[d * n_z + k].astype(jnp.float32)
+
+    for d in range(1, n_x):
+        for k in turns:
+            at = (d - 1) * n_z + k
+            to_x[at] = paired(d, k).astype(to_x.dtype)
+            send(to_x.at[at], from_x.at[at], x_sems, at, (x + d) % n_x, c, z)
+    for k in turns:
+        value = paired(0, k)
+        for d in range(1, n_x):
+            at = (d - 1) * n_z + k
+            push(to_x.at[at], from_x.at[at], x_sems, at, (x + d) % n_x, c, z).wait_recv()
+            value = value + from_x[at].astype(jnp.float32)
+        if k:
+            to_z[k - 1] = value.astype(to_z.dtype)
+            send(to_z.at[k - 1], from_z.at[k - 1], z_sems, k - 1, x, c, (z + k) % n_z)
+    for k in range(1, n_z):
+        push(to_z.at[k - 1], from_z.at[k - 1], z_sems, k - 1, x, c, (z + k) % n_z).wait_recv()
+        value = value + from_z[k - 1].astype(jnp.float32)
+    out_ref[...] = (own_ref[...].astype(jnp.float32) + value).astype(out_ref.dtype)
+    for copy in sends:
+        copy.wait_send()
+
+
+def scatter(part, own):
+    n_x, n_z = lax.axis_size("ep") // 2, lax.axis_size("tp")
+    rows, width = own.shape
+    sems = pltpu.SemaphoreType.DMA
+    held = [pltpu.VMEM((count, rows, width), part.dtype) for count in
+            (n_x * n_z, (n_x - 1) * n_z, (n_x - 1) * n_z, n_z - 1, n_z - 1)]
+    return pl.pallas_call(
+        scatter_kernel,
+        out_shape=jax.ShapeDtypeStruct(own.shape, own.dtype),
+        in_specs=[pl.BlockSpec(memory_space=pltpu.VMEM)] * 2,
+        out_specs=pl.BlockSpec(memory_space=pltpu.VMEM),
+        scratch_shapes=held + [sems((n_x * n_z,))] * 4 + [sems((n_z,))] * 2,
+        compiler_params=pltpu.CompilerParams(
+            collective_id=1, has_side_effects=True, vmem_limit_bytes=60 * 2**20
+        ),
+    )(part.reshape(n_x, 2, n_z, rows, width), own)
+
+
 def shards(hidden_states, norm_gain, expert_ids, gate_weights, capacity, expert_in, expert_out):
     token_count, width = hidden_states.shape
     expert_count = capacity.shape[0]
@@ -99,14 +254,12 @@
     low = (gates - high.astype(jnp.float32)).astype(jnp.bfloat16)
     pad = jnp.zeros((token_count, 128 - 2 * expert_count), jnp.bfloat16)
     sent = jnp.concatenate([normed, high, low, pad], axis=1)
-    gathered = lax.all_gather(sent, ("ep", "tp"), axis=0, tiled=True)
-    x = gathered[:, :width]
+    gathered = gather(sent)
     high = gathered[:, width : width + expert_count].astype(jnp.float32)
     low = gathered[:, width + expert_count : width + 2 * expert_count].astype(jnp.float32)
     mine = lax.dynamic_slice_in_dim(high + low, lax.axis_index("ep") * local_count, local_count, 1)
-    part = experts(x, mine.T, expert_in, expert_out)
-    summed = lax.psum_scatter(part, ("ep", "tp"), scatter_dimension=0, tiled=True)
-    return (values + summed.astype(jnp.float32)).astype(jnp.bfloat16)
+    part = experts(gathered, width, mine.T, expert_in, expert_out)
+    return scatter(part, hidden_states)
 
 
 def solution(mesh):

time: 168 us -> 95.2 us (0.57)
  waiting for transfers between devices: 103 us -> 0 us
  Pallas kernels: 40.1 us -> 87 us
  between operations: 13.5 us -> 0.06 us
    reduce_scatter x1 -> x0, waiting for transfers between devices: 59.8 us -> none  [shards(): lax.psum_scatter(part, ('ep', 'tp'), scatter_dimension=0, tiled=True)]
    pallas_call x0 -> x2, Pallas kernels: none -> 47 us  [the longest x1 24.1 us: gather(): pl.pallas_call(gather_kernel, out_shape=jax.ShapeDtypeStruct((n_x, 2, n_z...]
    all_gather x1 -> x0, waiting for transfers between devices: 43.5 us -> none  [shards(): gathered = lax.all_gather(sent, ('ep', 'tp'), axis=0, tiled=True)]
    slice x1 -> x0, local copies, waits for them, and re-layouts: 2.83 us -> none  [shards(): x = gathered[:, :width]]
  transfers between devices with their start and end apart: 2 -> 0, of which waited for: 2 -> 0; matrix products, arithmetic and copies ran while one was open for 0% -> 0% of each run, Pallas kernels for 0% -> 0%
where the time goes in v2:
time: 95.2 us; the launch traced here: 94.9 us
  Pallas kernels  87 us (91%)
  other arithmetic  4.15 us (4%)
  local copies, waits for them, and re-layouts  3.45 us (4%)
    pallas_call x1, Pallas kernels, experts(): pl.pallas_call(experts_kernel, grid=(count // ROWS, n_e, n_f // block), o...  40 us
    pallas_call x1, Pallas kernels, gather(): pl.pallas_call(gather_kernel, out_shape=jax.ShapeDtypeStruct((n_x, 2, n_z...  24.1 us
    pallas_call x1, Pallas kernels, scatter(): pl.pallas_call(scatter_kernel, out_shape=jax.ShapeDtypeStruct(own.shape,...  22.9 us

profile of v2, /device:TPU:0, one launch (start us, length us, event | category | flops | bytes accessed | tf_op | source)
XLA Modules:
  0.0 94.9 jit_solution(16164286065483655949)
XLA Ops:
  0.0 0.7 convert_element_type.31
  0.7 1.1 %fusion.1 = f32[8]{0:T(128)S(1)} fusion(bf16[8,7168]{1,0:T(8,128)(2,1)} %own_ref.1), kind=kLoop, calls=%fused_computation.4 | loop fusion | flops 172024 | bytes 114720 | tf_op jit(solution)/shard_map/reduce_sum | solution.py:244
  1.7 0.8 convert_reduce_fusion
  2.5 0.2 subtract_convert_fusion
  2.7 1.0 %fusion.3 = bf16[8,7168]{1,0:T(8,128)(2,1)S(1)} fusion(bf16[8,7168]{1,0:T(8,128)(2,1)} %own_ref.1, f32[7168]{0:T(1024)} %param.8, f32[8]{0:T(128)S(1)} %add_rsqrt_fusion), kind=kLoop, calls=%fused_computation.6 | loop fusion | flops 229376 | bytes 258080 | tf_op jit(solution)/shard_map/convert_element_type | solution.py:245
  3.8 0.7 concatenate.3.own_ref
  4.5 24.1 %shard_map.73 = bf16[2,2,4,8,7296]{4,3,2,1,0:T(8,128)(2,1)} custom-call(bf16[8,7296]{1,0:T(8,128)(2,1)} %concatenate.3.own_ref), custom_call_target="tpu_custom_call" | custom-call | tf_op jit(solution)/shard_map/pallas_call | solution.py:160
  28.6 0.9 fusion.10
  29.5 0.1 constant_dynamic-slice_fusion
  29.6 0.1 copy.16
  29.6 0.1 copy.17
  29.7 0.6 add_bitcast_fusion.w_ref
  30.3 40.0 %shard_map.74 = bf16[128,7168]{1,0:T(8,128)(2,1)} custom-call(bf16[128,7296]{1,0:T(8,128)(2,1)} %bitcast.6, f32[4,128]{1,0:T(4,128)} %add_bitcast_fusion.w_ref, bf16[4,512,2,7168]{3,2,1,0:T(2,128)(2,1)} %in_hbm.1, bf16[4,512,7168]{2,1,0:T(8,128)(2,1)} %out_w_ref.1), custom_call_target="tpu_custom_call" | custom-call | tf_op jit(solution)/shard_map/pallas_call | solution.py:62
  70.4 22.9 %shard_map.75 = bf16[8,7168]{1,0:T(8,128)(2,1)} custom-call(bf16[2,2,4,8,7168]{4,3,2,1,0:T(8,128)(2,1)} %bitcast.7, bf16[8,7168]{1,0:T(8,128)(2,1)} %own_ref.1), custom_call_target="tpu_custom_call" | custom-call | tf_op jit(solution)/shard_map/pallas_call | solution.py:227
  93.3 1.6 %copy.19 = bf16[8,7168]{1,0:T(8,128)(2,1)} copy(bf16[8,7168]{1,0:T(8,128)(2,1)} %shard_map.75) | data formatting | bytes 229376
  (3 shorter events, 0.0 us)
